TPU v7x, 32 devices: a whole 2x2x4 slice. The times are simulated.
32 devices in a mesh: grp: 2 (over y), ep: 4 (over x, core), hid: 4 (over z).
Axes of the slice: x: 2, y: 2, z: 4, core: 2. Of those that a mesh axis runs over, the one named last changes fastest.
Arguments:
- tokens: bfloat16 [1024, 4096], P(('grp', 'ep')), parts along dimension 0, may hold values from -6 to 6
- expert_ids: int32 [1024, 2], P(('grp', 'ep')), parts along dimension 0, may hold values from 0 to 3, all different within a row; in each aligned block of 128 rows (0 to 127, 128 to 255, ...) at most 64 rows name the same one
- gate_probs: float32 [1024, 2], P(('grp', 'ep')), parts along dimension 0, may hold values from 0.05 to 1
- w_gate: bfloat16 [16, 4096, 384], P(('ep', 'hid')), may hold values from -0.09375 to 0.09375
- w_up: bfloat16 [16, 4096, 384], P(('ep', 'hid')), may hold values from -0.09375 to 0.09375
- w_down: bfloat16 [16, 384, 4096], P(('ep', 'hid')), may hold values from -0.15625 to 0.15625
Outputs:
- mixed_out: bfloat16 [1024, 4096], P(('grp', 'ep'), 'hid'), parts along dimension 0
There are 2 independent parts, one for each index of `grp`. A program takes and returns all parts, laid end to end along the dimension named above; an argument that names none is the same for every part. Nothing has to cross between parts.
Inputs may be any that keep to these rules, and one draw needn't show every extreme that they name: `expert_ids`: each token names 2 different experts. Among the 128 tokens of one index of ep (aligned blocks of rows) no expert is named by more than 64 tokens, and in every draw some expert is named by exactly 64 tokens of some block.
All inputs are finite; a program needn't handle non-finite values.
Results may differ from a plain program's by a relative error of at most 0.0085.
Values may be sent and summed in bfloat16 or wider, within the bound.
A program may use at most 128 MiB of HBM per device.

v0:
```python
import functools

import jax
import jax.numpy as jnp
from jax import lax
from jax.experimental import pallas as pl
from jax.experimental.pallas import tpu as pltpu
from jax.sharding import PartitionSpec as P

QUARTERS = 4
ROW_CHUNKS = 4
RETURN_STEP = 128
MESH = pl.DeviceIdType.MESH
F32 = jnp.float32
BF16 = jnp.bfloat16


def kernel(ep_count, hid_count, tokens, ids, probs, w_gate, w_up, w_down, out,
           gate_buf, up_buf, down_buf, key_t, combine, outgoing, sibling_out, slots, hidden,
           partial, returned, owner_out, owner_in,
           weight_sem, disp_send, disp_recv, fwd_send, fwd_recv, ret_send, ret_recv, sum_send, sum_recv):
    ep = lax.axis_index("ep")
    hid = lax.axis_index("hid")
    groups = hid_count // QUARTERS
    group = hid // QUARTERS
    rows, width = tokens.shape
    picks = ids.shape[0]
    cap = slots.shape[1]
    half = width // 2
    pairs = ep_count // 2
    pair = ep // 2
    core = ep % 2
    sibling = pair * 2 + 1 - core
    mate = hid + 1 - 2 * (hid % 2)
    my_half = pl.ds(pl.multiple_of((hid % 2) * half, half), half)
    piece = cap // ROW_CHUNKS
    feat = width // hid_count
    chunks = partial.shape[0]
    step = feat // chunks

    loads = [pltpu.make_async_copy(src.at[0], dst, weight_sem.at[i])
             for i, (src, dst) in enumerate(((w_gate, gate_buf), (w_up, up_buf), (w_down, down_buf)))]
    for load in loads:
        load.start()

    barrier = pltpu.get_barrier_semaphore()
    for off in range(1, ep_count):
        pl.semaphore_signal(barrier, 1, device_id={"ep": lax.rem(ep + off, ep_count)}, device_id_type=MESH)
    for off in range(1, hid_count):
        pl.semaphore_signal(barrier, 1, device_id={"hid": lax.rem(hid + off, hid_count)}, device_id_type=MESH)

    name = lax.broadcasted_iota(jnp.int32, (128, rows), 0) * groups + group
    count = jnp.zeros((128, rows), F32)
    weight = jnp.zeros((128, rows), F32)
    gate_round = probs[...].astype(BF16).astype(F32)
    for k in range(picks):
        hit = ids[k:k + 1, :] == name
        count = jnp.where(hit, 1.0, count)
        weight = jnp.where(hit, gate_round[k:k + 1, :], weight)
    earlier = (lax.broadcasted_iota(jnp.int32, (rows, rows), 0)
               < lax.broadcasted_iota(jnp.int32, (rows, rows), 1)).astype(F32).astype(BF16)
    before = jnp.dot(count.astype(BF16), earlier, preferred_element_type=F32)
    place = jnp.where(count > 0.5, before, -1000.0)
    key_t[...] = place.astype(jnp.int32)

    def pick_rows(first, blocks):
        row = lax.broadcasted_iota(jnp.int32, (cap, rows), 0)
        parts = [(key_t[pl.ds(first + b, 1), :] == row).astype(F32).astype(BF16) for b in range(blocks)]
        return jnp.concatenate(parts, axis=0) if blocks > 1 else parts[0]

    tile = min(half, 512)
    sends = []
    for off in range(1, pairs):
        other = lax.rem(pair + off, pairs)
        chosen = pick_rows(2 * other, 2)
        for col in range(0, half, tile):
            src = pl.ds(pl.multiple_of((hid % 2) * half + col, tile), tile)
            rows_out = jnp.dot(chosen, tokens[:, src], preferred_element_type=F32).astype(BF16)
            outgoing[off - 1, :, :, col:col + tile] = rows_out.reshape(2, cap, tile)
    pl.semaphore_wait(barrier, ep_count - 1 + hid_count - 1)
    for off in range(1, pairs):
        other = lax.rem(pair + off, pairs)
        for r in range(ROW_CHUNKS):
            part = pl.ds(r * piece, piece)
            for flip in range(2):
                who = core if flip == 0 else 1 - core
                copy = pltpu.make_async_remote_copy(
                    src_ref=outgoing.at[off - 1, who, part],
                    dst_ref=slots.at[ep, part, my_half],
                    send_sem=disp_send.at[off, r, flip],
                    recv_sem=disp_recv.at[ep, r],
                    device_id={"ep": 2 * other + who}, device_id_type=MESH)
                copy.start()
                sends.append(copy)

    for col in range(0, width, tile):
        sibling_out[:, col:col + tile] = jnp.dot(
            pick_rows(sibling, 1), tokens[:, col:col + tile], preferred_element_type=F32).astype(BF16)
    to_sibling = pltpu.make_async_remote_copy(
        src_ref=sibling_out, dst_ref=slots.at[ep],
        send_sem=disp_send.at[0, 0, 0], recv_sem=disp_recv.at[ep, 0],
        device_id={"ep": sibling}, device_id_type=MESH)
    to_sibling.start()
    sends.append(to_sibling)
    for col in range(0, width, tile):
        slots[ep, :, col:col + tile] = jnp.dot(
            pick_rows(ep, 1), tokens[:, col:col + tile], preferred_element_type=F32).astype(BF16)

    lanes = lax.broadcasted_iota(jnp.int32, (rows, cap), 1)
    key = place.T.astype(jnp.int32)
    weight = weight.T
    for b in range(ep_count):
        combine[:, b * cap:(b + 1) * cap] = jnp.where(
            key[:, b:b + 1] == lanes, weight[:, b:b + 1], 0.0).astype(BF16)

    def act(which):
        block = slots[pl.ds(2 * which, 2)].reshape(2 * cap, width)
        gate_act = jnp.dot(block, gate_buf[...], preferred_element_type=F32)
        up_act = jnp.dot(block, up_buf[...], preferred_element_type=F32)
        value = gate_act / (1.0 + jnp.exp(-gate_act)) * up_act
        hidden[pl.ds(pl.multiple_of(which * 2 * cap, 2 * cap), 2 * cap), :] = value.astype(BF16)

    pltpu.make_async_remote_copy(
        src_ref=sibling_out, dst_ref=slots.at[sibling],
        send_sem=disp_send.at[0, 0, 0], recv_sem=disp_recv.at[sibling, 0],
        device_id={"ep": sibling}, device_id_type=MESH).wait_recv()
    loads[0].wait()
    loads[1].wait()
    act(pair)

    forwards = []
    for off in range(1, pairs):
        other = lax.rem(pair + pairs - off, pairs)
        for r in range(ROW_CHUNKS):
            part = pl.ds(r * piece, piece)
            for flip in range(2):
                source = 2 * other + (core if flip == 0 else 1 - core)
                landed = slots.at[source, part, my_half]
                pltpu.make_async_remote_copy(
                    src_ref=landed, dst_ref=landed,
                    send_sem=disp_send.at[off, r, flip], recv_sem=disp_recv.at[source, r],
                    device_id={"ep": source}, device_id_type=MESH).wait_recv()
                copy = pltpu.make_async_remote_copy(
                    src_ref=landed, dst_ref=landed,
                    send_sem=fwd_send.at[off, r, flip], recv_sem=fwd_recv.at[off, r, flip],
                    device_id={"hid": mate}, device_id_type=MESH)
                copy.start()
                forwards.append(copy)
    per = 2 * ROW_CHUNKS
    for off in range(1, pairs):
        for copy in forwards[(off - 1) * per:off * per]:
            copy.wait_recv()
        act(lax.rem(pair + pairs - off, pairs))

    loads[2].wait()
    for c in range(chunks):
        for h in range(hid_count):
            col = h * feat + c * step
            value = jnp.dot(hidden[...], down_buf[:, col:col + step], preferred_element_type=F32)
            partial[c, :, :, h * step:(h + 1) * step] = value.astype(BF16).reshape(ep_count, cap, step)
        for off in list(range(2, ep_count)) + [1]:
            owner = lax.rem(ep + off, ep_count)
            copy = pltpu.make_async_remote_copy(
                src_ref=partial.at[c, owner], dst_ref=returned.at[c, ep],
                send_sem=ret_send.at[c, off], recv_sem=ret_recv.at[c, ep],
                device_id={"ep": owner}, device_id_type=MESH)
            copy.start()
            sends.append(copy)
        returned[c, ep] = partial[c, ep]

    for c in range(chunks):
        for off in range(1, ep_count):
            source = lax.rem(ep + off, ep_count)
            pltpu.make_async_remote_copy(
                src_ref=partial.at[c, source], dst_ref=returned.at[c, source],
                send_sem=ret_send.at[c, off], recv_sem=ret_recv.at[c, source],
                device_id={"ep": source}, device_id_type=MESH).wait_recv()
        for h in range(hid_count):
            block = returned[c, :, :, h * step:(h + 1) * step].reshape(ep_count * cap, step)
            owner_out[c, h] = jnp.dot(combine[...], block, preferred_element_type=F32).astype(BF16)
        for off in list(range(2, hid_count)) + [1]:
            target = lax.rem(hid + off, hid_count)
            copy = pltpu.make_async_remote_copy(
                src_ref=owner_out.at[c, target], dst_ref=owner_in.at[c, hid],
                send_sem=sum_send.at[c, off], recv_sem=sum_recv.at[c, hid],
                device_id={"hid": target}, device_id_type=MESH)
            copy.start()
            sends.append(copy)

    for c in range(chunks):
        total = owner_out[c, hid].astype(F32)
        for off in range(1, hid_count):
            source = lax.rem(hid + off, hid_count)
            pltpu.make_async_remote_copy(
                src_ref=owner_out.at[c, source], dst_ref=owner_in.at[c, source],
                send_sem=sum_send.at[c, off], recv_sem=sum_recv.at[c, source],
                device_id={"hid": source}, device_id_type=MESH).wait_recv()
            total = total + owner_in[c, source].astype(F32)
        out[:, c * step:(c + 1) * step] = total.astype(BF16)
    for copy in sends + forwards:
        copy.wait_send()


def local(ep_count, hid_count, tokens, expert_ids, gate_probs, w_gate, w_up, w_down):
    rows, width = tokens.shape
    inner = w_gate.shape[2]
    cap = rows // 2
    feat = width // hid_count
    step = RETURN_STEP
    chunks = feat // step
    others = max(ep_count // 2 - 1, 1)
    vmem = pl.BlockSpec(memory_space=pltpu.VMEM)
    hbm = pl.BlockSpec(memory_space=pl.ANY)
    dma = pltpu.SemaphoreType.DMA
    return pl.pallas_call(
        functools.partial(kernel, ep_count, hid_count),
        out_shape=jax.ShapeDtypeStruct((rows, feat), BF16),
        in_specs=[vmem, vmem, vmem, hbm, hbm, hbm],
        out_specs=vmem,
        scratch_shapes=[
            pltpu.VMEM((width, inner), BF16),
            pltpu.VMEM((width, inner), BF16),
            pltpu.VMEM((inner, width), BF16),
            pltpu.VMEM((128, rows), jnp.int32),
            pltpu.VMEM((rows, ep_count * cap), BF16),
            pltpu.VMEM((others, 2, cap, width // 2), BF16),
            pltpu.VMEM((cap, width), BF16),
            pltpu.VMEM((ep_count, cap, width), BF16),
            pltpu.VMEM((ep_count * cap, inner), BF16),
            pltpu.VMEM((chunks, ep_count, cap, hid_count * step), BF16),
            pltpu.VMEM((chunks, ep_count, cap, hid_count * step), BF16),
            pltpu.VMEM((chunks, hid_count, rows, step), BF16),
            pltpu.VMEM((chunks, hid_count, rows, step), BF16),
            dma((3,)),
            dma((ep_count // 2, ROW_CHUNKS, 2)),
            dma((ep_count, ROW_CHUNKS)),
            dma((ep_count // 2, ROW_CHUNKS, 2)),
            dma((ep_count // 2, ROW_CHUNKS, 2)),
            dma((chunks, ep_count)),
            dma((chunks, ep_count)),
            dma((chunks, hid_count)),
            dma((chunks, hid_count)),
        ],
        compiler_params=pltpu.CompilerParams(
            collective_id=0, has_side_effects=True, vmem_limit_bytes=60 * 2**20),
    )(tokens, expert_ids.T, gate_probs.T, w_gate, w_up, w_down)


def solution(mesh):
    in_specs = (
        P(("grp", "ep"), None),
        P(("grp", "ep"), None),
        P(("grp", "ep"), None),
        P(("ep", "hid"), None, None),
        P(("ep", "hid"), None, None),
        P(("ep", "hid"), None, None),
    )
    out_specs = P(("grp", "ep"), "hid")
    body = functools.partial(local, mesh.shape["ep"], mesh.shape["hid"])
    return jax.shard_map(body, mesh=mesh, in_specs=in_specs, out_specs=out_specs, check_vma=False)
```

profile of v0, /device:TPU:1, one launch (start us, length us, event | category | flops | bytes accessed | tf_op | source)
XLA Modules:
  0.0 57.4 jit_solution(11646693916112906472)
XLA Ops:
  0.0 55.8 %shard_map.64 = bf16[128,1024]{1,0:T(8,128)(2,1)} custom-call(bf16[128,4096]{1,0:T(8,128)(2,1)} %tokens.1, s32[2,128]{1,0:T(2,128)} %bitcast.2, f32[2,128]{1,0:T(2,128)} %bitcast.3, bf16[1,4096,384]{2,1,0:T(8,128)(2,1)} %w_gate.1, bf16[1,4096,384]{2,1,0:T(8,128)(2,1)} %w_up.1, bf16[1,384,4096]{2,1,0:T(8,128)(2,1)} %w_down.1), custom_call_target="tpu_custom_call" | custom-call | tf_op jit(solution)/shard_map/pallas_call | solution.py:215
  55.8 1.7 %copy.8 = bf16[128,1024]{1,0:T(8,128)(2,1)} copy(bf16[128,1024]{1,0:T(8,128)(2,1)} %shard_map.64) | data formatting | bytes 524288
where the time goes:
time: 57.6 us; the launch traced here: 57.4 us
  Pallas kernels  55.8 us (97%)
  local copies, waits for them, and re-layouts  1.67 us (3%)
    pallas_call x1, Pallas kernels, local(): pl.pallas_call(functools.partial(kernel, ep_count, hid_count), out_shape=...  55.8 us
    unnamed x1, local copies, waits for them, and re-layouts  1.67 us

commit v1 on v0

v1 whole, which is shorter than its diff:
```python
import functools

import jax
import jax.numpy as jnp
from jax import lax
from jax.experimental import pallas as pl
from jax.experimental.pallas import tpu as pltpu
from jax.sharding import PartitionSpec as P

QUARTERS = 4
IN_CHUNKS = 4
HAND_OVER = 1
HELD_BACK = 2
RETURN_STEP = 256
MESH = pl.DeviceIdType.MESH
F32 = jnp.float32
BF16 = jnp.bfloat16


def aligned(index, size):
    return pl.ds(pl.multiple_of(index * size, size), size)


def kernel(ep_count, hid_count, tokens_hbm, ids_hbm, probs_hbm, w_gate, w_up, w_down, out,
           tokens, ids, probs, gate_buf, up_buf, down_buf, key_t, combine, outgoing, sibling_out, slots,
           gate_acc, up_acc, hidden, partial, returned, mate_out, mate_in, far_out, far_in,
           load_sem, sib_sem, disp_send, disp_recv, fwd_send, fwd_recv, ret_send, ret_sib, ret_recv,
           mate_send, mate_recv, far_send, far_recv):
    ep = lax.axis_index("ep")
    hid = lax.axis_index("hid")
    groups = hid_count // QUARTERS
    group = hid // QUARTERS
    rows, width = tokens.shape
    picks = ids.shape[0]
    cap = slots.shape[1]
    half = width // 2
    pairs = ep_count // 2
    pair = ep // 2
    core = ep % 2
    sibling = pair * 2 + 1 - core
    side = hid % 2
    mate = hid + 1 - 2 * side
    columns = hid_count // 2
    column = hid // 2
    feat = width // hid_count
    chunks, step = returned.shape[1], returned.shape[4]
    wide = half // IN_CHUNKS

    barrier = pltpu.get_barrier_semaphore()
    for off in range(1, ep_count):
        pl.semaphore_signal(barrier, 1, device_id={"ep": lax.rem(ep + off, ep_count)}, device_id_type=MESH)
    pl.semaphore_signal(barrier, 1, device_id={"hid": mate}, device_id_type=MESH)
    for off in range(1, columns):
        pl.semaphore_signal(barrier, 1, device_id={"hid": lax.rem(hid + 2 * off, hid_count)}, device_id_type=MESH)

    loads = [pltpu.make_async_copy(src, dst, load_sem.at[i])
             for i, (src, dst) in enumerate(((ids_hbm, ids), (probs_hbm, probs), (tokens_hbm, tokens),
                                             (w_gate.at[0], gate_buf), (w_up.at[0], up_buf), (w_down.at[0], down_buf)))]
    for load in loads[:3]:
        load.start()
    loads[0].wait()
    loads[1].wait()

    name = lax.broadcasted_iota(jnp.int32, (128, rows), 0) * groups + group
    count = jnp.zeros((128, rows), F32)
    weight = jnp.zeros((128, rows), F32)
    gate_round = probs[...].astype(BF16).astype(F32)
    for k in range(picks):
        hit = ids[k:k + 1, :] == name
        count = jnp.where(hit, 1.0, count)
        weight = jnp.where(hit, gate_round[k:k + 1, :], weight)
    earlier = (lax.broadcasted_iota(jnp.int32, (rows, rows), 0)
               < lax.broadcasted_iota(jnp.int32, (rows, rows), 1)).astype(F32).astype(BF16)
    before = jnp.dot(count.astype(BF16), earlier, preferred_element_type=F32)
    place = jnp.where(count > 0.5, before, -1000.0)
    key_t[...] = place.astype(jnp.int32)

    def pick_rows(first, blocks):
        row = lax.broadcasted_iota(jnp.int32, (cap, rows), 0)
        parts = [(key_t[pl.ds(first + b, 1), :] == row).astype(F32).astype(BF16) for b in range(blocks)]
        return jnp.concatenate(parts, axis=0) if blocks > 1 else parts[0]

    loads[2].wait()
    for load in loads[3:]:
        load.start()
    others = [lax.rem(pair + off, pairs) for off in range(1, pairs)]
    for i, other in enumerate(others):
        chosen = pick_rows(2 * other, 2)
        for k in range(IN_CHUNKS):
            rows_out = jnp.dot(chosen, tokens[:, aligned(side * IN_CHUNKS + k, wide)], preferred_element_type=F32)
            outgoing[i, :, :, k * wide:(k + 1) * wide] = rows_out.astype(BF16).reshape(2, cap, wide)
    dispatch = [pltpu.make_async_remote_copy(
        src_ref=outgoing.at[i, to, :, pl.ds(k * wide, wide)],
        dst_ref=slots.at[ep, :, aligned(side * IN_CHUNKS + k, wide)],
        send_sem=disp_send.at[to, i, k], recv_sem=disp_recv.at[ep, k],
        device_id={"ep": 2 * other + to}, device_id_type=MESH)
        for k in range(IN_CHUNKS) for i, other in enumerate(others) for to in range(2)]
    pl.semaphore_wait(barrier, ep_count - 1 + 1 + columns - 1)

    @pl.when(core == 0)
    def _():
        for copy in dispatch:
            copy.start()

    sends = list(dispatch)
    tile = min(half, 512)
    chosen = pick_rows(sibling, 1)
    for col in range(0, width, tile):
        sibling_out[:, col:col + tile] = jnp.dot(
            chosen, tokens[:, col:col + tile], preferred_element_type=F32).astype(BF16)
    to_sibling = pltpu.make_async_remote_copy(
        src_ref=sibling_out, dst_ref=slots.at[ep], send_sem=sib_sem.at[0], recv_sem=sib_sem.at[1],
        device_id={"ep": sibling}, device_id_type=MESH)
    to_sibling.start()
    sends.append(to_sibling)
    chosen = pick_rows(ep, 1)
    for col in range(0, width, tile):
        slots[ep, :, col:col + tile] = jnp.dot(
            chosen, tokens[:, col:col + tile], preferred_element_type=F32).astype(BF16)

    lanes = lax.broadcasted_iota(jnp.int32, (rows, cap), 1)
    key = place.T.astype(jnp.int32)
    weight = weight.T
    for b in range(ep_count):
        combine[:, b * cap:(b + 1) * cap] = jnp.where(
            key[:, b:b + 1] == lanes, weight[:, b:b + 1], 0.0).astype(BF16)

    def activation(gate_act, up_act):
        return (gate_act / (1.0 + jnp.exp(-gate_act)) * up_act).astype(BF16)

    def act_step(stage, i, k, first=False, last=False):
        block = slots[2 * others[i] + stage, :, aligned(k, wide)]
        gate_act = jnp.dot(block, gate_buf[aligned(k, wide), :], preferred_element_type=F32)
        up_act = jnp.dot(block, up_buf[aligned(k, wide), :], preferred_element_type=F32)
        if not first:
            gate_act = gate_act + gate_acc[stage, i]
            up_act = up_act + up_acc[stage, i]
        if last:
            hidden[stage, others[i]] = activation(gate_act, up_act)
        else:
            gate_acc[stage, i] = gate_act
            up_acc[stage, i] = up_act

    pltpu.make_async_remote_copy(
        src_ref=sibling_out, dst_ref=slots.at[sibling], send_sem=sib_sem.at[0], recv_sem=sib_sem.at[1],
        device_id={"ep": sibling}, device_id_type=MESH).wait_recv()
    loads[3].wait()
    loads[4].wait()
    block = slots[pl.ds(2 * pair, 2)].reshape(2 * cap, width)
    value = activation(jnp.dot(block, gate_buf[...], preferred_element_type=F32),
                       jnp.dot(block, up_buf[...], preferred_element_type=F32))
    for stage in range(2):
        hidden[stage, pair] = value[stage * cap:(stage + 1) * cap]

    def forward(stage, i, k):
        landed = slots.at[2 * others[i] + stage, :, aligned(side * IN_CHUNKS + k, wide)]
        return pltpu.make_async_remote_copy(
            src_ref=landed, dst_ref=landed,
            send_sem=fwd_send.at[i, k, stage], recv_sem=fwd_recv.at[i, k, stage],
            device_id={"hid": mate}, device_id_type=MESH)

    def direct(stage, i, k):
        source = 2 * others[i] + stage
        landed = slots.at[source, :, aligned(side * IN_CHUNKS + k, wide)]
        pltpu.make_async_remote_copy(
            src_ref=landed, dst_ref=landed,
            send_sem=disp_send.at[0, i, k], recv_sem=disp_recv.at[source, k],
            device_id={"ep": source}, device_id_type=MESH).wait_recv()
        copy = forward(stage, i, k)
        copy.start()
        sends.append(copy)
        act_step(stage, i, side * IN_CHUNKS + k, first=k == 0)

    def relayed(stage, i, k):
        forward(stage, i, k).wait_recv()
        act_step(stage, i, (1 - side) * IN_CHUNKS + k, last=k == IN_CHUNKS - 1)

    pieces = [(i, k) for i in range(pairs - 1) for k in range(IN_CHUNKS)]

    elsewhere = [lax.rem(column + off, columns) for off in range(1, columns)]
    targets = [2 * c + 1 - side for c in elsewhere] + [2 * c + side for c in elsewhere] + [mate, hid]

    def give_back(stage):
        for s, target in enumerate(targets):
            for c in range(chunks):
                value = jnp.dot(hidden[stage].reshape(pairs * cap, -1), down_buf[:, aligned(target * chunks + c, step)],
                                preferred_element_type=F32)
                partial[stage, s, c] = value.astype(BF16).reshape(pairs, cap, step)
                for i, other in enumerate(others):
                    copy = pltpu.make_async_remote_copy(
                        src_ref=partial.at[stage, s, c, other], dst_ref=returned.at[s, c, ep],
                        send_sem=ret_send.at[stage, s, c, i], recv_sem=ret_recv.at[s, c, ep],
                        device_id={"ep": 2 * other + stage}, device_id_type=MESH)
                    copy.start()
                    sends.append(copy)

        @pl.when(core == stage)
        def _():
            for s in range(hid_count):
                for c in range(chunks):
                    returned[s, c, ep] = partial[stage, s, c, pair]

        @pl.when(core != stage)
        def _():
            for s in range(hid_count):
                for c in range(chunks):
                    back_to_sibling(stage, s, c).start()

    def back_to_sibling(stage, s, c):
        return pltpu.make_async_remote_copy(
            src_ref=partial.at[stage, s, c, pair], dst_ref=returned.at[s, c, ep],
            send_sem=ret_sib.at[s, c], recv_sem=ret_recv.at[s, c, ep],
            device_id={"ep": sibling}, device_id_type=MESH)

    for n, piece in enumerate(pieces):
        direct(0, *piece)
        if n == HAND_OVER:
            @pl.when(core == 1)
            def _():
                for copy in dispatch:
                    copy.start()
    held = len(pieces) - HELD_BACK
    for n, piece in enumerate(pieces):
        relayed(0, *piece)
        if n < held:
            direct(1, *pieces[n])
    loads[5].wait()
    give_back(0)
    for piece in pieces[held:]:
        direct(1, *piece)
    for piece in pieces:
        relayed(1, *piece)
    give_back(1)

    def to_mate(slot, c):
        return pltpu.make_async_remote_copy(
            src_ref=mate_out.at[slot, c], dst_ref=mate_in.at[slot, c],
            send_sem=mate_send.at[slot, c], recv_sem=mate_recv.at[slot, c],
            device_id={"hid": mate}, device_id_type=MESH)

    def to_far(slot, c, target):
        return pltpu.make_async_remote_copy(
            src_ref=far_out.at[slot, c], dst_ref=far_in.at[slot, c],
            send_sem=far_send.at[slot, c], recv_sem=far_recv.at[slot, c],
            device_id={"hid": target}, device_id_type=MESH)

    for s, target in enumerate(targets):
        for c in range(chunks):
            for off in range(1, ep_count):
                source = lax.rem(ep + off, ep_count)
                pltpu.make_async_remote_copy(
                    src_ref=returned.at[s, c, source], dst_ref=returned.at[s, c, source],
                    send_sem=ret_sib.at[s, c], recv_sem=ret_recv.at[s, c, source],
                    device_id={"ep": source}, device_id_type=MESH).wait_recv()
            total = jnp.dot(combine[...], returned[s, c].reshape(ep_count * cap, step), preferred_element_type=F32)
            if s < columns - 1 or s == 2 * columns - 2:
                slot = s if s < columns - 1 else columns - 1
                mate_out[slot, c] = total.astype(BF16)
                copy = to_mate(slot, c)
            elif s < 2 * columns - 2:
                slot = s - (columns - 1)
                to_mate(slot, c).wait_recv()
                far_out[slot, c] = (total + mate_in[slot, c].astype(F32)).astype(BF16)
                copy = to_far(slot, c, target)
            else:
                to_mate(columns - 1, c).wait_recv()
                total = total + mate_in[columns - 1, c].astype(F32)
                for slot in range(columns - 1):
                    to_far(slot, c, target).wait_recv()
                    total = total + far_in[slot, c].astype(F32)
                out[:, c * step:(c + 1) * step] = total.astype(BF16)
                continue
            copy.start()
            sends.append(copy)
    for s in range(hid_count):
        for c in range(chunks):
            back_to_sibling(1 - core, s, c).wait_send()
    for copy in sends:
        copy.wait_send()


def local(ep_count, hid_count, tokens, expert_ids, gate_probs, w_gate, w_up, w_down):
    rows, width = tokens.shape
    inner = w_gate.shape[2]
    picks = expert_ids.shape[1]
    cap = rows // 2
    feat = width // hid_count
    step = min(RETURN_STEP, feat)
    chunks = feat // step
    pairs = ep_count // 2
    columns = hid_count // 2
    others = max(pairs - 1, 1)
    far = max(columns - 1, 1)
    hbm = pl.BlockSpec(memory_space=pl.ANY)
    dma = pltpu.SemaphoreType.DMA
    return pl.pallas_call(
        functools.partial(kernel, ep_count, hid_count),
        out_shape=pltpu.VMEM((rows, feat), BF16),
        in_specs=[hbm] * 6,
        out_specs=pl.BlockSpec(memory_space=pltpu.VMEM),
        scratch_shapes=[
            pltpu.VMEM((rows, width), BF16),
            pltpu.VMEM((picks, rows), jnp.int32),
            pltpu.VMEM((picks, rows), F32),
            pltpu.VMEM((width, inner), BF16),
            pltpu.VMEM((width, inner), BF16),
            pltpu.VMEM((inner, width), BF16),
            pltpu.VMEM((128, rows), jnp.int32),
            pltpu.VMEM((rows, ep_count * cap), BF16),
            pltpu.VMEM((others, 2, cap, width // 2), BF16),
            pltpu.VMEM((cap, width), BF16),
            pltpu.VMEM((ep_count, cap, width), BF16),
            pltpu.VMEM((2, others, cap, inner), F32),
            pltpu.VMEM((2, others, cap, inner), F32),
            pltpu.VMEM((2, pairs, cap, inner), BF16),
            pltpu.VMEM((2, hid_count, chunks, pairs, cap, step), BF16),
            pltpu.VMEM((hid_count, chunks, ep_count, cap, step), BF16),
            pltpu.VMEM((columns, chunks, rows, step), BF16),
            pltpu.VMEM((columns, chunks, rows, step), BF16),
            pltpu.VMEM((far, chunks, rows, step), BF16),
            pltpu.VMEM((far, chunks, rows, step), BF16),
            dma((6,)),
            dma((2,)),
            dma((2, others, IN_CHUNKS)),
            dma((ep_count, IN_CHUNKS)),
            dma((others, IN_CHUNKS, 2)),
            dma((others, IN_CHUNKS, 2)),
            dma((2, hid_count, chunks, others)),
            dma((hid_count, chunks)),
            dma((hid_count, chunks, ep_count)),
            dma((columns, chunks)),
            dma((columns, chunks)),
            dma((far, chunks)),
            dma((far, chunks)),
        ],
        compiler_params=pltpu.CompilerParams(
            collective_id=0, has_side_effects=True, vmem_limit_bytes=60 * 2**20),
    )(tokens, expert_ids.T, gate_probs.T, w_gate, w_up, w_down)


def solution(mesh):
    in_specs = (
        P(("grp", "ep"), None),
        P(("grp", "ep"), None),
        P(("grp", "ep"), None),
        P(("ep", "hid"), None, None),
        P(("ep", "hid"), None, None),
        P(("ep", "hid"), None, None),
    )
    out_specs = P(("grp", "ep"), "hid")
    body = functools.partial(local, mesh.shape["ep"], mesh.shape["hid"])
    return jax.shard_map(body, mesh=mesh, in_specs=in_specs, out_specs=out_specs, check_vma=False)
```

time: 57.6 us -> 50.1 us (0.87)
  Pallas kernels: 55.8 us -> 49.2 us
  local copies, waits for them, and re-layouts: 1.67 us -> 0.71 us
    pallas_call x1, Pallas kernels: 55.8 us -> 49.2 us  [local(): pl.pallas_call(functools.partial(kernel, ep_count, hid_count), out_shape=...]
    unnamed x1, local copies, waits for them, and re-layouts: 1.67 us -> 0.71 us
where the time goes in v1:
time: 50.1 us; the launch traced here: 49.9 us
  Pallas kernels  49.2 us (98%)
  local copies, waits for them, and re-layouts  0.71 us (1%)
    pallas_call x1, Pallas kernels, local(): pl.pallas_call(functools.partial(kernel, ep_count, hid_count), out_shape=...  49.2 us

profile of v1, /device:TPU:1, one launch (start us, length us, event | category | flops | bytes accessed | tf_op | source)
XLA Modules:
  0.0 49.9 jit_solution(152653424867948180)
XLA Ops:
  0.0 49.2 %shard_map.64 = bf16[128,1024]{1,0:T(8,128)(2,1)S(1)} custom-call(bf16[128,4096]{1,0:T(8,128)(2,1)} %tokens_hbm.1, s32[2,128]{1,0:T(2,128)} %bitcast.2, f32[2,128]{1,0:T(2,128)} %bitcast.3, bf16[1,4096,384]{2,1,0:T(8,128)(2,1)} %w_gate.1, bf16[1,4096,384]{2,1,0:T(8,128)(2,1)} %w_up.1, bf16[1,384,4096]{2,1,0:T(8,128)(2,1)} %w_down.1), custom_call_target="tpu_custom_call" | custom-call | tf_op jit(solution)/shard_map/pallas_call | solution.py:296
  49.2 0.7 %copy.8 = bf16[128,1024]{1,0:T(8,128)(2,1)} copy(bf16[128,1024]{1,0:T(8,128)(2,1)S(1)} %shard_map.64) | data formatting | bytes 524288

commit v2 on v1

--- a/solution.py
+++ b/solution.py
@@ -11,6 +11,7 @@
 IN_CHUNKS = 4
 HAND_OVER = 1
 HELD_BACK = 2
+EARLY = (8, 4)
 RETURN_STEP = 256
 MESH = pl.DeviceIdType.MESH
 F32 = jnp.float32
@@ -180,37 +181,84 @@
     elsewhere = [lax.rem(column + off, columns) for off in range(1, columns)]
     targets = [2 * c + 1 - side for c in elsewhere] + [2 * c + side for c in elsewhere] + [mate, hid]
 
-    def give_back(stage):
-        for s, target in enumerate(targets):
-            for c in range(chunks):
-                value = jnp.dot(hidden[stage].reshape(pairs * cap, -1), down_buf[:, aligned(target * chunks + c, step)],
-                                preferred_element_type=F32)
-                partial[stage, s, c] = value.astype(BF16).reshape(pairs, cap, step)
-                for i, other in enumerate(others):
-                    copy = pltpu.make_async_remote_copy(
-                        src_ref=partial.at[stage, s, c, other], dst_ref=returned.at[s, c, ep],
-                        send_sem=ret_send.at[stage, s, c, i], recv_sem=ret_recv.at[s, c, ep],
-                        device_id={"ep": 2 * other + stage}, device_id_type=MESH)
-                    copy.start()
-                    sends.append(copy)
+    away = [(s, c) for s in range(columns - 1) for c in range(chunks)]
+    for c in range(chunks):
+        away += [(s, c) for s in range(columns - 1, 2 * columns - 1)]
+    own = [(hid_count - 1, c) for c in range(chunks)]
+
+    def give_back(stage, order):
+        for s, c in order:
+            target = targets[s]
+            value = jnp.dot(hidden[stage].reshape(pairs * cap, -1), down_buf[:, aligned(target * chunks + c, step)],
+                            preferred_element_type=F32)
+            partial[stage, s, c] = value.astype(BF16).reshape(pairs, cap, step)
+            for i, other in enumerate(others):
+                copy = pltpu.make_async_remote_copy(
+                    src_ref=partial.at[stage, s, c, other], dst_ref=returned.at[s, c, ep],
+                    send_sem=ret_send.at[stage, s, c, i], recv_sem=ret_recv.at[s, c, ep],
+                    device_id={"ep": 2 * other + stage}, device_id_type=MESH)
+                copy.start()
+                sends.append(copy)
 
         @pl.when(core == stage)
         def _():
-            for s in range(hid_count):
-                for c in range(chunks):
-                    returned[s, c, ep] = partial[stage, s, c, pair]
+            for s, c in order:
+                returned[s, c, ep] = partial[stage, s, c, pair]
 
         @pl.when(core != stage)
         def _():
-            for s in range(hid_count):
-                for c in range(chunks):
-                    back_to_sibling(stage, s, c).start()
+            for s, c in order:
+                back_to_sibling(stage, s, c).start()
 
     def back_to_sibling(stage, s, c):
         return pltpu.make_async_remote_copy(
             src_ref=partial.at[stage, s, c, pair], dst_ref=returned.at[s, c, ep],
             send_sem=ret_sib.at[s, c], recv_sem=ret_recv.at[s, c, ep],
             device_id={"ep": sibling}, device_id_type=MESH)
+
+    def to_mate(slot, c):
+        return pltpu.make_async_remote_copy(
+            src_ref=mate_out.at[slot, c], dst_ref=mate_in.at[slot, c],
+            send_sem=mate_send.at[slot, c], recv_sem=mate_recv.at[slot, c],
+            device_id={"hid": mate}, device_id_type=MESH)
+
+    def to_far(slot, c, target):
+        return pltpu.make_async_remote_copy(
+            src_ref=far_out.at[slot, c], dst_ref=far_in.at[slot, c],
+            send_sem=far_send.at[slot, c], recv_sem=far_recv.at[slot, c],
+            device_id={"hid": target}, device_id_type=MESH)
+
+    def gather(s, c):
+        for off in range(1, ep_count):
+            source = lax.rem(ep + off, ep_count)
+            pltpu.make_async_remote_copy(
+                src_ref=returned.at[s, c, source], dst_ref=returned.at[s, c, source],
+                send_sem=ret_sib.at[s, c], recv_sem=ret_recv.at[s, c, source],
+                device_id={"ep": source}, device_id_type=MESH).wait_recv()
+        total = jnp.dot(combine[...], returned[s, c].reshape(ep_count * cap, step), preferred_element_type=F32)
+        if s < columns - 1 or s == 2 * columns - 2:
+            slot = s if s < columns - 1 else columns - 1
+            mate_out[slot, c] = total.astype(BF16)
+            copy = to_mate(slot, c)
+        elif s < 2 * columns - 2:
+            slot = s - (columns - 1)
+            to_mate(slot, c).wait_recv()
+            far_out[slot, c] = (total + mate_in[slot, c].astype(F32)).astype(BF16)
+            copy = to_far(slot, c, targets[s])
+        else:
+            to_mate(columns - 1, c).wait_recv()
+            total = total + mate_in[columns - 1, c].astype(F32)
+            for slot in range(columns - 1):
+                to_far(slot, c, targets[s]).wait_recv()
+                total = total + far_in[slot, c].astype(F32)
+            out[:, c * step:(c + 1) * step] = total.astype(BF16)
+            return
+        copy.start()
+    def gather_on(which, order):
+        @pl.when(core == which)
+        def _():
+            for s, c in order:
+                gather(s, c)
 
     for n, piece in enumerate(pieces):
         direct(0, *piece)
@@ -225,56 +273,30 @@
         if n < held:
             direct(1, *pieces[n])
     loads[5].wait()
-    give_back(0)
+    give_back(0, away)
     for piece in pieces[held:]:
         direct(1, *piece)
+    first = EARLY[0]
+    gather_on(0, away[:first])
     for piece in pieces:
         relayed(1, *piece)
-    give_back(1)
-
-    def to_mate(slot, c):
-        return pltpu.make_async_remote_copy(
-            src_ref=mate_out.at[slot, c], dst_ref=mate_in.at[slot, c],
-            send_sem=mate_send.at[slot, c], recv_sem=mate_recv.at[slot, c],
-            device_id={"hid": mate}, device_id_type=MESH)
-
-    def to_far(slot, c, target):
-        return pltpu.make_async_remote_copy(
-            src_ref=far_out.at[slot, c], dst_ref=far_in.at[slot, c],
-            send_sem=far_send.at[slot, c], recv_sem=far_recv.at[slot, c],
-            device_id={"hid": target}, device_id_type=MESH)
-
-    for s, target in enumerate(targets):
-        for c in range(chunks):
-            for off in range(1, ep_count):
-                source = lax.rem(ep + off, ep_count)
-                pltpu.make_async_remote_copy(
-                    src_ref=returned.at[s, c, source], dst_ref=returned.at[s, c, source],
-                    send_sem=ret_sib.at[s, c], recv_sem=ret_recv.at[s, c, source],
-                    device_id={"ep": source}, device_id_type=MESH).wait_recv()
-            total = jnp.dot(combine[...], returned[s, c].reshape(ep_count * cap, step), preferred_element_type=F32)
-            if s < columns - 1 or s == 2 * columns - 2:
-                slot = s if s < columns - 1 else columns - 1
-                mate_out[slot, c] = total.astype(BF16)
-                copy = to_mate(slot, c)
-            elif s < 2 * columns - 2:
-                slot = s - (columns - 1)
-                to_mate(slot, c).wait_recv()
-                far_out[slot, c] = (total + mate_in[slot, c].astype(F32)).astype(BF16)
-                copy = to_far(slot, c, target)
-            else:
-                to_mate(columns - 1, c).wait_recv()
-                total = total + mate_in[columns - 1, c].astype(F32)
-                for slot in range(columns - 1):
-                    to_far(slot, c, target).wait_recv()
-                    total = total + far_in[slot, c].astype(F32)
-                out[:, c * step:(c + 1) * step] = total.astype(BF16)
-                continue
-            copy.start()
-            sends.append(copy)
+    early = first + EARLY[1]
+    gather_on(0, away[first:early])
+    give_back(1, away)
+    give_back(0, own)
+    give_back(1, own)
+    gather_on(1, away[:early])
+    for s, c in away[early:] + own:
+        gather(s, c)
+
     for s in range(hid_count):
         for c in range(chunks):
             back_to_sibling(1 - core, s, c).wait_send()
+    for c in range(chunks):
+        for slot in range(columns):
+            to_mate(slot, c).wait_send()
+        for slot in range(columns - 1):
+            to_far(slot, c, targets[columns - 1 + slot]).wait_send()
     for copy in sends:
         copy.wait_send()
 

time: 50.1 us -> 44.3 us (0.88)
  Pallas kernels: 49.2 us -> 43.5 us
    pallas_call x1, Pallas kernels: 49.2 us -> 43.5 us  [local(): pl.pallas_call(functools.partial(kernel, ep_count, hid_count), out_shape=...]
where the time goes in v2:
time: 44.3 us; the launch traced here: 44.2 us
  Pallas kernels  43.5 us (98%)
  local copies, waits for them, and re-layouts  0.71 us (2%)
    pallas_call x1, Pallas kernels, local(): pl.pallas_call(functools.partial(kernel, ep_count, hid_count), out_shape=...  43.5 us

profile of v2, /device:TPU:1, one launch (start us, length us, event | category | flops | bytes accessed | tf_op | source)
XLA Modules:
  0.0 44.2 jit_solution(14886787245908209115)
XLA Ops:
  0.0 43.5 %shard_map.64 = bf16[128,1024]{1,0:T(8,128)(2,1)S(1)} custom-call(bf16[128,4096]{1,0:T(8,128)(2,1)} %tokens_hbm.1, s32[2,128]{1,0:T(2,128)} %bitcast.2, f32[2,128]{1,0:T(2,128)} %bitcast.3, bf16[1,4096,384]{2,1,0:T(8,128)(2,1)} %w_gate.1, bf16[1,4096,384]{2,1,0:T(8,128)(2,1)} %w_up.1, bf16[1,384,4096]{2,1,0:T(8,128)(2,1)} %w_down.1), custom_call_target="tpu_custom_call" | custom-call | tf_op jit(solution)/shard_map/pallas_call | solution.py:318
  43.5 0.7 %copy.8 = bf16[128,1024]{1,0:T(8,128)(2,1)} copy(bf16[128,1024]{1,0:T(8,128)(2,1)S(1)} %shard_map.64) | data formatting | bytes 524288

commit v3 on v2

--- a/solution.py
+++ b/solution.py
@@ -11,7 +11,7 @@
 IN_CHUNKS = 4
 HAND_OVER = 1
 HELD_BACK = 2
-EARLY = (8, 4)
+EARLY = (10, 2)
 RETURN_STEP = 256
 MESH = pl.DeviceIdType.MESH
 F32 = jnp.float32
@@ -26,7 +26,7 @@
            tokens, ids, probs, gate_buf, up_buf, down_buf, key_t, combine, outgoing, sibling_out, slots,
            gate_acc, up_acc, hidden, partial, returned, mate_out, mate_in, far_out, far_in,
            load_sem, sib_sem, disp_send, disp_recv, fwd_send, fwd_recv, ret_send, ret_sib, ret_recv,
-           mate_send, mate_recv, far_send, far_recv):
+           mate_send, mate_recv, far_send, far_recv, here):
     ep = lax.axis_index("ep")
     hid = lax.axis_index("hid")
     groups = hid_count // QUARTERS
@@ -51,8 +51,16 @@
     for off in range(1, ep_count):
         pl.semaphore_signal(barrier, 1, device_id={"ep": lax.rem(ep + off, ep_count)}, device_id_type=MESH)
     pl.semaphore_signal(barrier, 1, device_id={"hid": mate}, device_id_type=MESH)
-    for off in range(1, columns):
-        pl.semaphore_signal(barrier, 1, device_id={"hid": lax.rem(hid + 2 * off, hid_count)}, device_id_type=MESH)
+    relay = columns == 2
+    across = jnp.clip(hid - 1 + 2 * side, 0, hid_count - 1)
+    inner = (hid > 0) & (hid < hid_count - 1)
+    if relay:
+        @pl.when(inner)
+        def _():
+            pl.semaphore_signal(barrier, 1, device_id={"hid": across}, device_id_type=MESH)
+    else:
+        for off in range(1, columns):
+            pl.semaphore_signal(barrier, 1, device_id={"hid": lax.rem(hid + 2 * off, hid_count)}, device_id_type=MESH)
 
     loads = [pltpu.make_async_copy(src, dst, load_sem.at[i])
              for i, (src, dst) in enumerate(((ids_hbm, ids), (probs_hbm, probs), (tokens_hbm, tokens),
@@ -85,23 +93,30 @@
     for load in loads[3:]:
         load.start()
     others = [lax.rem(pair + off, pairs) for off in range(1, pairs)]
-    for i, other in enumerate(others):
-        chosen = pick_rows(2 * other, 2)
-        for k in range(IN_CHUNKS):
-            rows_out = jnp.dot(chosen, tokens[:, aligned(side * IN_CHUNKS + k, wide)], preferred_element_type=F32)
-            outgoing[i, :, :, k * wide:(k + 1) * wide] = rows_out.astype(BF16).reshape(2, cap, wide)
     dispatch = [pltpu.make_async_remote_copy(
         src_ref=outgoing.at[i, to, :, pl.ds(k * wide, wide)],
         dst_ref=slots.at[ep, :, aligned(side * IN_CHUNKS + k, wide)],
         send_sem=disp_send.at[to, i, k], recv_sem=disp_recv.at[ep, k],
         device_id={"ep": 2 * other + to}, device_id_type=MESH)
         for k in range(IN_CHUNKS) for i, other in enumerate(others) for to in range(2)]
-    pl.semaphore_wait(barrier, ep_count - 1 + 1 + columns - 1)
-
-    @pl.when(core == 0)
-    def _():
-        for copy in dispatch:
-            copy.start()
+    chosen = [pick_rows(2 * other, 2) for other in others]
+    for k in range(IN_CHUNKS):
+        for i in range(pairs - 1):
+            rows_out = jnp.dot(chosen[i], tokens[:, aligned(side * IN_CHUNKS + k, wide)], preferred_element_type=F32)
+            outgoing[i, :, :, k * wide:(k + 1) * wide] = rows_out.astype(BF16).reshape(2, cap, wide)
+        if k == 0:
+            pl.semaphore_wait(barrier, ep_count + (inner.astype(jnp.int32) if relay else columns - 1))
+
+        @pl.when(core == 0)
+        def _():
+            for copy in dispatch[2 * (pairs - 1) * k:2 * (pairs - 1) * (k + 1)]:
+                copy.start()
+
+    if relay:
+        @pl.when(inner)
+        def _():
+            pl.semaphore_signal(here, 1, device_id={"hid": across}, device_id_type=MESH)
+            pl.semaphore_signal(here, 1, device_id={"hid": mate}, device_id_type=MESH)
 
     sends = list(dispatch)
     tile = min(half, 512)
@@ -273,6 +288,8 @@
         if n < held:
             direct(1, *pieces[n])
     loads[5].wait()
+    if relay:
+        pl.semaphore_wait(here, 1)
     give_back(0, away)
     for piece in pieces[held:]:
         direct(1, *piece)
@@ -354,6 +371,7 @@
             dma((columns, chunks)),
             dma((far, chunks)),
             dma((far, chunks)),
+            pltpu.SemaphoreType.REGULAR,
         ],
         compiler_params=pltpu.CompilerParams(
             collective_id=0, has_side_effects=True, vmem_limit_bytes=60 * 2**20),

time: 44.3 us -> 44.4 us (level)
  no operation moved by 1% of the time
where the time goes in v3:
time: 44.4 us; the launch traced here: 44.2 us
  Pallas kernels  43.5 us (98%)
  local copies, waits for them, and re-layouts  0.71 us (2%)
    pallas_call x1, Pallas kernels, local(): pl.pallas_call(functools.partial(kernel, ep_count, hid_count), out_shape=...  43.5 us

profile of v3, /device:TPU:1, one launch (start us, length us, event | category | flops | bytes accessed | tf_op | source)
XLA Modules:
  0.0 44.2 jit_solution(1623468589750011660)
XLA Ops:
  0.0 43.5 %shard_map.64 = bf16[128,1024]{1,0:T(8,128)(2,1)S(1)} custom-call(bf16[128,4096]{1,0:T(8,128)(2,1)} %tokens_hbm.1, s32[2,128]{1,0:T(2,128)} %bitcast.2, f32[2,128]{1,0:T(2,128)} %bitcast.3, bf16[1,4096,384]{2,1,0:T(8,128)(2,1)} %w_gate.1, bf16[1,4096,384]{2,1,0:T(8,128)(2,1)} %w_up.1, bf16[1,384,4096]{2,1,0:T(8,128)(2,1)} %w_down.1), custom_call_target="tpu_custom_call" | custom-call | tf_op jit(solution)/shard_map/pallas_call | solution.py:335
  43.5 0.7 %copy.8 = bf16[128,1024]{1,0:T(8,128)(2,1)} copy(bf16[128,1024]{1,0:T(8,128)(2,1)S(1)} %shard_map.64) | data formatting | bytes 524288
